TPU v7x, 32 devices: a whole 2x2x4 slice. The times are simulated.
32 devices in a mesh: groups: 2 (over y), expert: 4 (over x, core), tensor: 4 (over z).
Axes of the slice: x: 2, y: 2, z: 4, core: 2. Of those that a mesh axis runs over, the one named last changes fastest.
Arguments:
- tokens: bfloat16 [512, 4096], P(('groups', 'expert'), 'tensor'), parts along dimension 0, may hold values from -400 to 400
- norm_gain: float32 [4096], replicated, may hold values from 0.5 to 1.5
- w_gate: bfloat16 [4096, 65536], P(None, ('expert', 'tensor')), may hold values from -0.09375 to 0.09375
- w_up: bfloat16 [4096, 65536], P(None, ('expert', 'tensor')), may hold values from -0.09375 to 0.09375
- w_down: bfloat16 [65536, 4096], P(('expert', 'tensor')), may hold values from -0.0625 to 0.0625
- expert_ids: int32 [512, 2], P(('groups', 'expert')), parts along dimension 0, may hold values from 0 to 7, all different within a row; in each aligned block of 64 rows (0 to 63, 64 to 127, ...) at most 32 rows name the same one
- gate_weights: float32 [512, 2], P(('groups', 'expert')), parts along dimension 0, may hold values from 0.1 to 1
Outputs:
- moe_out: bfloat16 [512, 4096], P(('groups', 'expert'), 'tensor'), parts along dimension 0
There are 2 independent parts, one for each index of `groups`. A program takes and returns all parts, laid end to end along the dimension named above; an argument that names none is the same for every part. Nothing has to cross between parts.
Inputs may be any that keep to these rules, and one draw needn't show every extreme that they name: `expert_ids`: each request names two different experts. Within the rows of one device (aligned blocks of 64 rows) no expert is named by more than 32 rows, and in some blocks one expert is named by exactly 32 rows.
All inputs are finite; a program needn't handle non-finite values.
Results may differ from a plain program's by a relative error of at most 0.008.
Values may be sent and summed in bfloat16 or wider, within the bound.
A program may use at most 192 MiB of HBM per device.

v0:
```python
import functools

import jax
import jax.numpy as jnp
from jax import lax
from jax.experimental import pallas as pl
from jax.experimental.pallas import tpu as pltpu
from jax.sharding import PartitionSpec as P

EXPERTS = 8
MIB = 1 << 20
MESH = pl.DeviceIdType.MESH


def log2(value):
    power = value.bit_length() - 1
    assert 1 << power == value
    return power


def kernel(
    n_e, n_t, cap, chunk, pair_slots, lag,
    tokens, gain, meta, ids, w_gate, w_up, w_down,
    out,
    wbuf, blocks, metas, packed, hidden, wslot, place, sendbuf, recvbuf, zsend, zrecv,
    wsem, lsem, rsem, zsem, xsem, dsem, msend, mrecv, osend, orecv, ysend, yrecv,
):
    g, e, t = lax.axis_index("groups"), lax.axis_index("expert"), lax.axis_index("tensor")
    n_x = n_e // 2
    xi, core = e // 2, e % 2
    sibling = xi * 2 + (1 - core)
    rows, width_local = tokens.shape
    width = w_gate.shape[0]
    hid = w_gate.shape[1]
    per_expert = n_e * n_t // EXPERTS
    mine = (e * n_t + t) // per_expert
    gate_pairs = hid // chunk
    per_slice = width_local // chunk
    down_chunks = n_t * per_slice
    pairs = gate_pairs + down_chunks // 2

    def slice_of(s):
        return lax.rem(t + 1 + s, n_t)

    def weight_copy(src, slot):
        return pltpu.make_async_copy(src, wbuf.at[slot, pl.ds(0, src.shape[0])], wsem.at[slot])

    def columns(start, size):
        return pl.ds(pl.multiple_of(start, size), size)

    def down_columns(d):
        return columns(slice_of(d // per_slice) * width_local + (d % per_slice) * chunk, chunk)

    def start_pair(p):
        slot = (p % pair_slots) * 2

        @pl.when(p < gate_pairs)
        def _():
            cols = columns(p * chunk, chunk)
            weight_copy(w_gate.at[:, cols], slot).start()
            weight_copy(w_up.at[:, cols], slot + 1).start()

        @pl.when(jnp.logical_and(p >= gate_pairs, p < pairs))
        def _():
            d = (p - gate_pairs) * 2
            weight_copy(w_down.at[:, down_columns(d)], slot).start()
            weight_copy(w_down.at[:, down_columns(d + 1)], slot + 1).start()

    def block_copy(ej, q, send_sem, to):
        return pltpu.make_async_remote_copy(
            src_ref=blocks.at[ej, q], dst_ref=blocks.at[ej, q],
            send_sem=send_sem, recv_sem=rsem.at[ej, q], device_id=to, device_id_type=MESH,
        )

    def z_copy(side, q):
        return block_copy(e, q, zsem.at[side, q], (g, e, lax.rem(t + 1 - 2 * side + n_t, n_t)))

    def x_copy(o, q):
        return block_copy(e, q, xsem.at[o, q], (g, lax.rem(xi + o, n_x) * 2 + core, t))

    def d_copy(o, q):
        ej = lax.rem(xi + o, n_x) * 2 + core
        return block_copy(ej, q, dsem.at[o, q], (g, sibling, t))

    def arrived(ej, q):
        block_copy(ej, q, zsem.at[0, 0], (g, sibling, t)).wait_recv()

    def has_next(side):
        return t < n_t - 1 if side == 0 else t > 0

    def at_distance(h, step):
        for side in (0, 1):
            q = t - h if side == 0 else t + h

            @pl.when(q >= 0 if side == 0 else q < n_t)
            def _():
                step(side, q)

    def meta_copy(o):
        return pltpu.make_async_remote_copy(
            src_ref=meta, dst_ref=metas.at[e], send_sem=msend.at[o], recv_sem=mrecv.at[e],
            device_id=(g, lax.rem(e + o, n_e), t), device_id_type=MESH,
        )

    def meta_arrived(o):
        ej = lax.rem(e + o, n_e)
        pltpu.make_async_remote_copy(
            src_ref=meta, dst_ref=metas.at[ej], send_sem=msend.at[0], recv_sem=mrecv.at[ej],
            device_id=(g, ej, t), device_id_type=MESH,
        ).wait_recv()

    own = pltpu.make_async_copy(tokens, blocks.at[e, t], lsem.at[0])
    own.start()
    own_meta = pltpu.make_async_copy(meta, metas.at[e], lsem.at[1])
    own_meta.start()
    barrier = pltpu.get_barrier_semaphore()
    for o in range(1, n_e):
        pl.semaphore_signal(barrier, inc=1, device_id=(g, lax.rem(e + o, n_e), t), device_id_type=MESH)
    for o in range(1, n_t):
        pl.semaphore_signal(barrier, inc=1, device_id=(g, e, lax.rem(t + o, n_t)), device_id_type=MESH)
    for p in range(min(pair_slots, pairs)):
        start_pair(jnp.int32(p))
    own.wait()
    own_meta.wait()

    slots = n_e * cap
    column = lax.broadcasted_iota(jnp.int32, (rows, slots), 1)
    expert_at = ((column >> log2(cap)) * n_t + t) >> log2(per_expert)
    member = jnp.logical_or(ids[:, 0:1] == expert_at, ids[:, 1:2] == expert_at)
    before = lax.broadcasted_iota(jnp.int32, (rows, rows), 1) < lax.broadcasted_iota(jnp.int32, (rows, rows), 0)
    rank = jnp.dot(
        before.astype(jnp.float32).astype(jnp.bfloat16),
        member.astype(jnp.float32).astype(jnp.bfloat16),
        preferred_element_type=jnp.float32,
    )
    hit = jnp.logical_and(member, rank == (column & (cap - 1)).astype(jnp.float32))
    place[...] = hit.astype(jnp.float32).astype(jnp.bfloat16)

    pl.semaphore_wait(barrier, n_e - 1 + n_t - 1)

    for o in range(1, n_e):
        meta_copy(o).start()
    for side in (0, 1):
        @pl.when(has_next(side))
        def _():
            z_copy(side, t).start()

    lanes = meta.shape[1]
    upper = (
        lax.broadcasted_iota(jnp.int32, (lanes, lanes), 0) < lax.broadcasted_iota(jnp.int32, (lanes, lanes), 1)
    ).astype(jnp.float32).astype(jnp.bfloat16)

    def pick(ej):
        id0, id1 = metas[ej, 0:1, :], metas[ej, 1:2, :]
        target = mine.astype(jnp.float32)
        named = jnp.where(id0 == target, 1.0, 0.0) + jnp.where(id1 == target, 1.0, 0.0)
        order = jnp.dot(
            jnp.broadcast_to(named, (8, lanes)).astype(jnp.bfloat16), upper, preferred_element_type=jnp.float32
        )[0:1, :]
        slot = lax.broadcasted_iota(jnp.int32, (cap, lanes), 0).astype(jnp.float32)
        return jnp.where(slot == order, 1.0, 0.0) * named

    def pack(s):
        q = s

        def one(ej, _):
            @pl.when(ej % 2 != core)
            def _():
                arrived(ej, q)

            select = pick(ej)[:, :rows].astype(jnp.bfloat16)
            picked = jnp.dot(select, blocks[ej, q], preferred_element_type=jnp.float32)
            packed[columns(ej * cap, cap), columns(q * width_local, width_local)] = picked.astype(jnp.bfloat16)
            return 0

        lax.fori_loop(0, n_e, one, 0)

    def relay(s):
        for o in range(1, n_x):
            arrived(lax.rem(xi + o, n_x) * 2 + core, s)
            d_copy(o, s).start()

    def forward(s):
        for o in range(1, n_x):
            x_copy(o, s).start()
        d_copy(0, s).start()

    forward(t)
    for o in range(1, n_e):
        meta_arrived(o)

    def take(side, q):
        arrived(e, q)

        @pl.when(has_next(side))
        def _():
            z_copy(side, q).start()

        forward(q)

    def finish(side, q):
        relay(q)
        pack(q)

    at_distance(1, take)
    finish(0, t)

    def dispatch(h, _):
        at_distance(h, take)
        at_distance(h - 1, finish)
        return 0

    lax.fori_loop(2, n_t, dispatch, 0)
    at_distance(n_t - 1, finish)

    def normalize(ej, _):
        at = columns(ej * cap, cap)
        weight = jnp.where(metas[ej, 0:1, :] == mine.astype(jnp.float32), metas[ej, 2:3, :], metas[ej, 3:4, :])
        wslot[at, :] = jnp.broadcast_to(jnp.sum(pick(ej) * weight, axis=1, keepdims=True), (cap, lanes))
        values = packed[at, :].astype(jnp.float32)
        scale = lax.rsqrt(jnp.sum(values * values, axis=1, keepdims=True) / width + 1e-05)
        packed[at, :] = (values * scale * gain[...]).astype(jnp.bfloat16)
        return 0

    lax.fori_loop(0, n_e, normalize, 0)

    def expert_in(j, _):
        slot = (j % pair_slots) * 2
        cols = columns(j * chunk, chunk)
        weight_copy(w_gate.at[:, cols], slot).wait()
        gate = jnp.dot(packed[...], wbuf[slot], preferred_element_type=jnp.float32)
        weight_copy(w_up.at[:, cols], slot + 1).wait()
        up = jnp.dot(packed[...], wbuf[slot + 1], preferred_element_type=jnp.float32)
        hidden[:, cols] = (gate / (1.0 + jnp.exp(-gate)) * up).astype(jnp.bfloat16)
        start_pair(j + pair_slots)
        return 0

    lax.fori_loop(0, gate_pairs, expert_in, 0)

    def o_copy(o, d):
        ej = lax.rem(e + o, n_e)
        return pltpu.make_async_remote_copy(
            src_ref=sendbuf.at[d, columns(ej * cap, cap)], dst_ref=recvbuf.at[d, columns(e * cap, cap)],
            send_sem=osend.at[o, d], recv_sem=orecv.at[e, d], device_id=(g, ej, t), device_id_type=MESH,
        )

    def o_arrived(o, d):
        ej = lax.rem(e + o, n_e)
        pltpu.make_async_remote_copy(
            src_ref=sendbuf.at[d, columns(ej * cap, cap)], dst_ref=recvbuf.at[d, columns(ej * cap, cap)],
            send_sem=osend.at[0, 0], recv_sem=orecv.at[ej, d], device_id=(g, ej, t), device_id_type=MESH,
        ).wait_recv()

    def y_copy(d):
        k, c = d // per_slice, d % per_slice
        return pltpu.make_async_remote_copy(
            src_ref=zsend.at[d], dst_ref=zrecv.at[t, c],
            send_sem=ysend.at[d], recv_sem=yrecv.at[t, c],
            device_id=(g, e, slice_of(k)), device_id_type=MESH,
        )

    def y_arrived(s, c):
        tj = lax.rem(t + s, n_t)
        pltpu.make_async_remote_copy(
            src_ref=zsend.at[0], dst_ref=zrecv.at[tj, c],
            send_sem=ysend.at[0], recv_sem=yrecv.at[tj, c],
            device_id=(g, e, tj), device_id_type=MESH,
        ).wait_recv()
        return zrecv[tj, c].astype(jnp.float32)

    def combined(d):
        for o in range(1, n_e):
            o_arrived(o, d)
        return jnp.dot(place[...], recvbuf[d], preferred_element_type=jnp.float32)

    def combine_and_send(d):
        zsend[d] = combined(d).astype(jnp.bfloat16)
        y_copy(d).start()

    def expert_out(d, _):
        slot = ((gate_pairs + d // 2) % pair_slots) * 2 + d % 2
        weight_copy(w_down.at[:, down_columns(d)], slot).wait()
        value = jnp.dot(hidden[...], wbuf[slot, 0:hid, :], preferred_element_type=jnp.float32)
        sendbuf[d] = (value * wslot[:, 0:1]).astype(jnp.bfloat16)
        for o in range(1, n_e):
            o_copy(o, d).start()
        at = columns(e * cap, cap)
        recvbuf[d, at, :] = sendbuf[d, at, :]

        @pl.when(d % 2 == 1)
        def _():
            start_pair(gate_pairs + d // 2 + pair_slots)

        @pl.when(jnp.logical_and(d >= lag, d - lag < down_chunks - per_slice))
        def _():
            combine_and_send(d - lag)

        return 0

    lax.fori_loop(0, down_chunks, expert_out, 0)

    def late(d, _):
        combine_and_send(d)
        return 0

    lax.fori_loop(max(0, down_chunks - lag), down_chunks - per_slice, late, 0)
    for c in range(per_slice):
        total = combined(down_chunks - per_slice + c)
        for s in range(1, n_t):
            total += y_arrived(s, c)
        out[:, c * chunk:(c + 1) * chunk] = total.astype(jnp.bfloat16)

    for o in range(1, n_e):
        meta_copy(o).wait_send()

    def drain_blocks(s, _):
        for side in (0, 1):
            @pl.when(jnp.logical_and(has_next(side), s <= t if side == 0 else s >= t))
            def _():
                z_copy(side, s).wait_send()

        for o in range(n_x):
            if o:
                x_copy(o, s).wait_send()
            d_copy(o, s).wait_send()
        return 0

    lax.fori_loop(0, n_t, drain_blocks, 0)

    def drain_rows(d, _):
        for o in range(1, n_e):
            o_copy(o, d).wait_send()
        return 0

    lax.fori_loop(0, down_chunks, drain_rows, 0)

    def drain_sums(d, _):
        y_copy(d).wait_send()
        return 0

    lax.fori_loop(0, down_chunks - per_slice, drain_sums, 0)


def per_device(n_e, n_t, tokens, norm_gain, w_gate, w_up, w_down, expert_ids, gate_weights):
    rows, width_local = tokens.shape
    width, hid = w_gate.shape
    cap = rows // 2
    slots = n_e * cap
    chunk = min(512, width_local, hid)
    per_slice = width_local // chunk
    down_chunks = n_t * per_slice
    pairs = hid // chunk + down_chunks // 2
    spent = 2 * (width * rows * n_e + slots * width + slots * hid + 2 * slots * width + 2 * rows * width)
    pair_slots = min(pairs, (56 * MIB - spent) // (4 * width * chunk))
    lanes = -(-rows // 128) * 128
    pad = lanes - rows
    meta = jnp.concatenate(
        [
            jnp.pad(expert_ids.T.astype(jnp.float32), ((0, 0), (0, pad)), constant_values=-1.0),
            jnp.pad(gate_weights.T, ((0, 4), (0, pad))),
        ],
        axis=0,
    )
    vmem = pl.BlockSpec(memory_space=pltpu.VMEM)
    hbm = pl.BlockSpec(memory_space=pl.ANY)
    bf16, f32, dma = jnp.bfloat16, jnp.float32, pltpu.SemaphoreType.DMA
    return pl.pallas_call(
        functools.partial(kernel, n_e, n_t, cap, chunk, pair_slots, 3),
        out_shape=jax.ShapeDtypeStruct((rows, width_local), bf16),
        in_specs=[vmem, vmem, vmem, vmem, hbm, hbm, hbm],
        out_specs=vmem,
        scratch_shapes=[
            pltpu.VMEM((2 * pair_slots, width, chunk), bf16),
            pltpu.VMEM((n_e, n_t, rows, width_local), bf16),
            pltpu.VMEM((n_e, 8, lanes), f32),
            pltpu.VMEM((slots, width), bf16),
            pltpu.VMEM((slots, hid), bf16),
            pltpu.VMEM((slots, lanes), f32),
            pltpu.VMEM((rows, slots), bf16),
            pltpu.VMEM((down_chunks, slots, chunk), bf16),
            pltpu.VMEM((down_chunks, slots, chunk), bf16),
            pltpu.VMEM((down_chunks, rows, chunk), bf16),
            pltpu.VMEM((n_t, per_slice, rows, chunk), bf16),
            dma((2 * pair_slots,)),
            dma((2,)),
            dma((n_e, n_t)),
            dma((2, n_t)),
            dma((n_e // 2, n_t)),
            dma((n_e // 2, n_t)),
            dma((n_e,)),
            dma((n_e,)),
            dma((n_e, down_chunks)),
            dma((n_e, down_chunks)),
            dma((down_chunks,)),
            dma((n_t, per_slice)),
        ],
        compiler_params=pltpu.CompilerParams(
            collective_id=0, has_side_effects=True, vmem_limit_bytes=67043328
        ),
    )(tokens, norm_gain.reshape(1, width), meta, expert_ids, w_gate, w_up, w_down)


def solution(mesh):
    in_specs = (
        P(("groups", "expert"), "tensor"),
        P(),
        P(None, ("expert", "tensor")),
        P(None, ("expert", "tensor")),
        P(("expert", "tensor"), None),
        P(("groups", "expert"), None),
        P(("groups", "expert"), None),
    )
    out_specs = P(("groups", "expert"), "tensor")
    body = functools.partial(per_device, mesh.shape["expert"], mesh.shape["tensor"])
    return jax.shard_map(body, mesh=mesh, in_specs=in_specs, out_specs=out_specs, check_vma=False)
```

profile of v0, /device:TPU:0, one launch (start us, length us, event | category | flops | bytes accessed | tf_op | source)
XLA Modules:
  0.0 59.6 jit_solution(11132469241953065448)
XLA Ops:
  0.0 0.7 %convert_bitcast_fusion = f32[2,64]{1,0:T(2,128)S(1)} fusion(s32[64,2]{0,1:T(2,128)} %param.12), kind=kLoop, calls=%fused_computation.3 | loop fusion | flops 128 | bytes 1024 | tf_op jit(solution)/shard_map/convert_element_type | solution.py:359
  0.7 1.3 %select_maximum_fusion.meta = f32[8,128]{1,0:T(8,128)} fusion(f32[2,64]{1,0:T(2,128)} %bitcast.5, f32[2,64]{1,0:T(2,128)S(1)} %convert_bitcast_fusion), kind=kLoop, calls=%fused_computation | loop fusion | flops 5120 | bytes 5120 | tf_op jit(solution)/shard_map/concatenate | solution.py:357
  2.0 1.4 %copy.8.ids = s32[64,2]{1,0:T(8,128)} copy(s32[64,2]{0,1:T(2,128)} %param.12) | data formatting | bytes 1024 | tf_op args[5]
  3.3 54.7 %shard_map.73 = bf16[64,1024]{1,0:T(8,128)(2,1)} custom-call(bf16[64,1024]{1,0:T(8,128)(2,1)} %tokens.1, f32[1,4096]{1,0:T(1,128)} %bitcast.4, f32[8,128]{1,0:T(8,128)} %select_maximum_fusion.meta, s32[64,2]{1,0:T(8,128)} %copy.8.ids, bf16[4096,4096]{1,0:T(8,128)(2,1)} %w_gate.1, bf16[4096,4096]{1,0:T(8,128)(2,1)} %w_up.1, bf16[4096,4096]{1,0:T(8,128)(2,1)} %w_down.1), custom_call_target="tpu_custom_call" | custom-call | tf_op jit(solution)/shard_map/pallas_call | solution.py:367
  58.0 1.6 %copy.10 = bf16[64,1024]{1,0:T(8,128)(2,1)} copy(bf16[64,1024]{1,0:T(8,128)(2,1)} %shard_map.73) | data formatting | bytes 262144
where the time goes:
time: 60.5 us; the launch traced here: 59.6 us
  Pallas kernels  54.7 us (90%)
  local copies, waits for them, and re-layouts  2.95 us (5%)
  other arithmetic  1.95 us (3%)
    pallas_call x1, Pallas kernels, per_device(): pl.pallas_call(functools.partial(kernel, n_e, n_t, cap, chunk, pair_slots...  54.7 us
    unnamed x2, local copies, waits for them, and re-layouts  2.95 us
    concatenate x1, other arithmetic, per_device(): jnp.concatenate([jnp.pad(expert_ids.T.astype(jnp.float32), ((0, 0), (0, p...  1.27 us

commit v1 on v0

v1 whole, which is shorter than its diff:
```python
import functools

import jax
import jax.numpy as jnp
from jax import lax
from jax.experimental import pallas as pl
from jax.experimental.pallas import tpu as pltpu
from jax.sharding import PartitionSpec as P

EXPERTS = 8
MIB = 1 << 20
MESH = pl.DeviceIdType.MESH
LANES = 128


def kernel(
    n_e, n_t, cap, ring, lag, pieces, dc,
    tokens, gain_in, ids_in, weights_in, w_gate, w_up, w_down,
    out,
    wbuf, blocks, gain, ids, weights, spread, place, wsend, wslot, sendpk, recvpk, packed, ssq, scale,
    acc_gate, acc_up, hidden,
    sendbuf, recvbuf, zsend, zrecv, outbuf,
    wsem, lsem, rsem, zsem, psend, precv, msend, mrecv, osend, orecv, ysend, yrecv,
):
    g, e, t = lax.axis_index("groups"), lax.axis_index("expert"), lax.axis_index("tensor")
    rows, kr = tokens.shape
    width = w_gate.shape[0]
    hid = w_gate.shape[1]
    sc = wbuf.shape[2]
    slots = n_e * cap
    per_expert = n_e * n_t // EXPERTS
    nj = hid // sc
    gate_units = n_t * nj
    parts = hid // kr
    per_slot = sc // dc
    per_slice = kr // dc
    down_chunks = n_t * per_slice
    units = gate_units + down_chunks
    kp = kr // pieces

    def order(s):
        return jnp.bitwise_xor(t, s)

    def slice_of(k):
        return order(2 * lax.rem(k // 2 + 1, n_t // 2) + 1 - lax.rem(k, 2))

    def columns(start, size):
        return pl.ds(pl.multiple_of(start, size), size)

    def down_columns(d):
        return columns(slice_of(d // per_slice) * kr + (d % per_slice) * dc, dc)

    def gate_copies(u, q, j):
        slot = lax.rem(u, ring) * 2
        at = (columns(q * kr, kr), columns(j * sc, sc))
        return (
            pltpu.make_async_copy(w_gate.at[at], wbuf.at[slot], wsem.at[slot, 0]),
            pltpu.make_async_copy(w_up.at[at], wbuf.at[slot + 1], wsem.at[slot + 1, 0]),
        )

    def down_copies(d):
        slot = lax.rem(gate_units + d, ring) * 2
        return [
            pltpu.make_async_copy(
                w_down.at[k * kr:(k + 1) * kr, down_columns(d)],
                wbuf.at[slot + k // per_slot, :, k % per_slot * dc:(k % per_slot + 1) * dc],
                wsem.at[slot + k // per_slot, k % per_slot],
            )
            for k in range(parts)
        ]

    def start_unit(u):
        @pl.when(u < gate_units)
        def _():
            for copy in gate_copies(u, order(u // nj), u % nj):
                copy.start()

        @pl.when(jnp.logical_and(u >= gate_units, u < units))
        def _():
            for copy in down_copies(u - gate_units):
                copy.start()

    def block_copy(q, p, send_sem, to):
        return pltpu.make_async_remote_copy(
            src_ref=blocks.at[q, p], dst_ref=blocks.at[q, p],
            send_sem=send_sem, recv_sem=rsem.at[q, p], device_id=(g, e, to), device_id_type=MESH,
        )

    def z_copy(j, p):
        return block_copy(t, p, zsem.at[j, p], order(j))

    def z_relay(s, p):
        return block_copy(order(s), p, zsem.at[s + 1, p], order(1))

    def rows_copy(src, dst, send_sem, recv_sem, o):
        ej = lax.rem(e + o, n_e)
        return pltpu.make_async_remote_copy(
            src_ref=src.at[columns(ej * cap, cap)], dst_ref=dst.at[columns(e * cap, cap)],
            send_sem=send_sem, recv_sem=recv_sem.at[e], device_id=(g, ej, t), device_id_type=MESH,
        )

    def rows_arrived(src, dst, send_sem, recv_sem, o):
        ej = lax.rem(e + o, n_e)
        at = columns(ej * cap, cap)
        pltpu.make_async_remote_copy(
            src_ref=src.at[at], dst_ref=dst.at[at],
            send_sem=send_sem, recv_sem=recv_sem.at[ej], device_id=(g, ej, t), device_id_type=MESH,
        ).wait_recv()

    def p_copy(o, q, p):
        return rows_copy(sendpk.at[q, p], recvpk.at[q, p], psend.at[o, q, p], precv.at[q, p], o)

    def m_copy(o):
        return rows_copy(wsend, wslot, msend.at[o], mrecv, o)

    own_rows = columns(e * cap, cap)

    local = [
        pltpu.make_async_copy(ids_in, ids, lsem.at[0]),
        pltpu.make_async_copy(weights_in, weights, lsem.at[1]),
        pltpu.make_async_copy(gain_in, gain, lsem.at[2]),
    ] + [
        pltpu.make_async_copy(tokens.at[:, p * kp:(p + 1) * kp], blocks.at[t, p], lsem.at[3 + p])
        for p in range(pieces)
    ]
    for copy in local:
        copy.start()
    barrier = pltpu.get_barrier_semaphore()
    for o in range(1, n_e):
        pl.semaphore_signal(barrier, inc=1, device_id=(g, lax.rem(e + o, n_e), t), device_id_type=MESH)
    for o in range(1, n_t):
        pl.semaphore_signal(barrier, inc=1, device_id=(g, e, lax.rem(t + o, n_t)), device_id_type=MESH)

    def prefetch(u, _):
        start_unit(u)
        return 0

    lax.fori_loop(0, min(ring, units), prefetch, 0)
    for copy in local:
        copy.wait()

    upper = (
        lax.broadcasted_iota(jnp.int32, (rows, rows), 0) < lax.broadcasted_iota(jnp.int32, (rows, rows), 1)
    ).astype(jnp.float32).astype(jnp.bfloat16)

    for ej in range(n_e):
        expert = (ej * n_t + t) // per_expert
        named = jnp.where(ids[0:1, :] == expert, 1.0, 0.0) + jnp.where(ids[1:2, :] == expert, 1.0, 0.0)
        rank = jnp.dot(
            jnp.broadcast_to(named, (8, rows)).astype(jnp.bfloat16), upper, preferred_element_type=jnp.float32
        )[0:1, :]
        slot = lax.broadcasted_iota(jnp.int32, (cap, rows), 0).astype(jnp.float32)
        hit = jnp.where(slot == rank, 1.0, 0.0) * named
        weight = jnp.where(ids[0:1, :] == expert, weights[0:1, :], weights[1:2, :])
        at = slice(ej * cap, (ej + 1) * cap)
        spread[at, :] = hit.astype(jnp.bfloat16)
        wsend[at, :] = jnp.broadcast_to(jnp.sum(hit * weight, axis=1, keepdims=True), (cap, LANES))
        filled = jnp.concatenate([hit, jnp.zeros((cap, LANES - rows), jnp.float32)], axis=1)
        place[:, at] = jnp.transpose(filled)[0:rows, :].astype(jnp.bfloat16)
    wslot[own_rows, :] = wsend[own_rows, :]
    ssq[...] = jnp.zeros_like(ssq)

    pl.semaphore_wait(barrier, n_e - 1 + n_t - 1)

    def dispatch(q, p):
        picked = jnp.dot(spread[...], blocks[q, p], preferred_element_type=jnp.float32)
        sendpk[q, p] = picked.astype(jnp.bfloat16)
        for o in range(1, n_e):
            p_copy(o, q, p).start()
        recvpk[q, p, own_rows, :] = sendpk[q, p, own_rows, :]

    def take(s):
        q = order(s)
        for p in range(pieces):
            block_copy(q, p, zsem.at[1, 0], order(1)).wait_recv()

            @pl.when(lax.rem(s, 2) == 0)
            def _():
                z_relay(s, p).start()

            dispatch(q, p)

    def pack(q):
        for p in range(pieces):
            for o in range(1, n_e):
                rows_arrived(sendpk.at[q, p], recvpk.at[q, p], psend.at[0, 0, 0], precv.at[q, p], o)
            gain_q = gain[:, columns(q * kr + p * kp, kp)]
            for r in range(slots // 32):
                at = slice(r * 32, (r + 1) * 32)
                value = recvpk[q, p, at, :].astype(jnp.float32)
                square = value * value
                total = square[:, 0:LANES]
                for c in range(1, kp // LANES):
                    total += square[:, c * LANES:(c + 1) * LANES]
                ssq[at, :] += total
                packed[p, at, :] = (value * gain_q).astype(jnp.bfloat16)

    def contract(ref, inner):
        value = jnp.dot(packed[0], ref[0:kp, inner], preferred_element_type=jnp.float32)
        for p in range(1, pieces):
            value += jnp.dot(packed[p], ref[p * kp:(p + 1) * kp, inner], preferred_element_type=jnp.float32)
        return value

    def expert_in(s, first, last):
        q = order(s)
        pack(q)
        if last:
            mean = jnp.sum(ssq[...], axis=1, keepdims=True) / width
            scale[...] = jnp.broadcast_to(lax.rsqrt(mean + 1e-05), scale.shape)

        def one(j, _):
            u = s * nj + j
            slot = lax.rem(u, ring) * 2
            if not last:
                @pl.when(j == nj // 2)
                def _():
                    @pl.when(s + 2 < n_t)
                    def _():
                        take(s + 2)

            for copy in gate_copies(u, q, j):
                copy.wait()
            wide = min(512, sc)
            for n in range(sc // wide):
                inner = slice(n * wide, (n + 1) * wide)
                at = columns(j * sc + n * wide, wide)
                gate = contract(wbuf.at[slot], inner)
                if not first:
                    gate += acc_gate[:, at]
                up = contract(wbuf.at[slot + 1], inner)
                if not first:
                    up += acc_up[:, at]
                if last:
                    for c in range(wide // LANES):
                        lanes = slice(c * LANES, (c + 1) * LANES)
                        gated = gate[:, lanes] * scale[...]
                        value = gated / (1.0 + jnp.exp(-gated)) * (up[:, lanes] * scale[...])
                        hidden[:, columns(j * sc + n * wide + c * LANES, LANES)] = value.astype(jnp.bfloat16)
                else:
                    acc_gate[:, at] = gate
                    acc_up[:, at] = up
            start_unit(u + ring)
            return 0

        lax.fori_loop(0, nj, one, 0)

    for p in range(pieces):
        z_copy(1, p).start()
    for j in range(2, n_t, 2):
        for p in range(pieces):
            z_copy(j, p).start()
    for p in range(pieces):
        dispatch(t, p)
    take(jnp.int32(1))
    expert_in(jnp.int32(0), True, False)

    def middle(s, _):
        expert_in(s, False, False)
        return 0

    lax.fori_loop(1, n_t - 1, middle, 0)
    for o in range(1, n_e):
        m_copy(o).start()
    expert_in(jnp.int32(n_t - 1), False, True)

    for o in range(1, n_e):
        rows_arrived(wsend, wslot, msend.at[0], mrecv, o)

    def o_copy(o, d):
        return rows_copy(sendbuf.at[d], recvbuf.at[d], osend.at[o, d], orecv.at[d], o)

    def o_arrived(o, d):
        rows_arrived(sendbuf.at[d], recvbuf.at[d], osend.at[0, 0], orecv.at[d], o)

    def pair_of(d):
        return lax.rem(d // per_slice // 2 + 1, n_t // 2), lax.rem(d, per_slice)

    def y_copy(d, far):
        m, c = pair_of(d)
        return pltpu.make_async_remote_copy(
            src_ref=zsend.at[d], dst_ref=zrecv.at[far, m, c],
            send_sem=ysend.at[d], recv_sem=yrecv.at[far, m, c],
            device_id=(g, e, order(2 * m if far else 1)), device_id_type=MESH,
        )

    def y_arrived(far, m, c):
        pltpu.make_async_remote_copy(
            src_ref=zsend.at[0], dst_ref=zrecv.at[far, m, c],
            send_sem=ysend.at[0], recv_sem=yrecv.at[far, m, c],
            device_id=(g, e, order(1)), device_id_type=MESH,
        ).wait_recv()
        return zrecv[far, m, c].astype(jnp.float32)

    def combined(d):
        for o in range(1, n_e):
            o_arrived(o, d)
        return jnp.dot(place[...], recvbuf[d], preferred_element_type=jnp.float32)

    def combine_and_send(d):
        total = combined(d)
        odd = lax.rem(d // per_slice, 2)

        @pl.when(odd == 0)
        def _():
            zsend[d] = total.astype(jnp.bfloat16)
            y_copy(d, 0).start()

        @pl.when(odd == 1)
        def _():
            zsend[d] = (total + y_arrived(0, *pair_of(d))).astype(jnp.bfloat16)
            y_copy(d, 1).start()

    def expert_out(d, _):
        slot = lax.rem(gate_units + d, ring) * 2
        for copy in down_copies(d):
            copy.wait()
        value = jnp.dot(hidden[:, 0:kr], wbuf[slot, :, 0:dc], preferred_element_type=jnp.float32)
        for k in range(1, parts):
            value += jnp.dot(
                hidden[:, k * kr:(k + 1) * kr],
                wbuf[slot + k // per_slot, :, k % per_slot * dc:(k % per_slot + 1) * dc],
                preferred_element_type=jnp.float32,
            )
        for c in range(dc // LANES):
            lanes = slice(c * LANES, (c + 1) * LANES)
            sendbuf[d, :, lanes] = (value[:, lanes] * wslot[...]).astype(jnp.bfloat16)
        for o in range(1, n_e):
            o_copy(o, d).start()
        recvbuf[d, own_rows, :] = sendbuf[d, own_rows, :]
        if gate_units + ring < units:
            start_unit(gate_units + d + ring)

        @pl.when(jnp.logical_and(d >= lag, d - lag < down_chunks - per_slice))
        def _():
            combine_and_send(d - lag)

        return 0

    lax.fori_loop(0, down_chunks, expert_out, 0)

    def late(d, _):
        combine_and_send(d)
        return 0

    lax.fori_loop(max(0, down_chunks - lag), down_chunks - per_slice, late, 0)
    results = []
    for c in range(per_slice):
        total = combined(down_chunks - per_slice + c)
        total += y_arrived(0, 0, c)
        for m in range(1, n_t // 2):
            total += y_arrived(1, m, c)
        outbuf[:, c * dc:(c + 1) * dc] = total.astype(jnp.bfloat16)
        done = pltpu.make_async_copy(
            outbuf.at[:, c * dc:(c + 1) * dc], out.at[:, c * dc:(c + 1) * dc], lsem.at[3 + pieces + c]
        )
        done.start()
        results.append(done)

    for o in range(1, n_e):
        m_copy(o).wait_send()

    for j in range(1, n_t):
        for p in range(pieces):
            z_copy(j, p).wait_send()

    def drain_blocks(s, _):
        for p in range(pieces):
            for o in range(1, n_e):
                p_copy(o, s, p).wait_send()
        return 0

    lax.fori_loop(0, n_t, drain_blocks, 0)

    def drain_rows(d, _):
        for o in range(1, n_e):
            o_copy(o, d).wait_send()
        return 0

    lax.fori_loop(0, down_chunks, drain_rows, 0)

    def drain_sums(d, _):
        y_copy(d, 0).wait_send()
        return 0

    lax.fori_loop(0, down_chunks - per_slice, drain_sums, 0)
    for done in results:
        done.wait()


def per_device(n_e, n_t, tokens, norm_gain, w_gate, w_up, w_down, expert_ids, gate_weights):
    rows, kr = tokens.shape
    width, hid = w_gate.shape
    cap = rows // 2
    slots = n_e * cap
    sc = min(1024, hid)
    dc = min(512, kr)
    pieces = 2
    assert n_t > 1 and n_t & (n_t - 1) == 0
    assert hid % kr == 0 and hid // kr <= 2 * (sc // dc)
    per_slice = kr // dc
    down_chunks = n_t * per_slice
    units = n_t * (hid // sc) + down_chunks
    spent = (
        6 * rows * width + 8 * slots * width + 2 * slots * kr + 10 * slots * hid
        + 18 * slots * LANES + 2 * rows * kr + MIB
    )
    ring = min(units, (63 * MIB + MIB // 2 - spent) // (4 * kr * sc))
    hbm = pl.BlockSpec(memory_space=pl.ANY)
    bf16, f32, i32, dma = jnp.bfloat16, jnp.float32, jnp.int32, pltpu.SemaphoreType.DMA
    return pl.pallas_call(
        functools.partial(kernel, n_e, n_t, cap, ring, 3, pieces, dc),
        out_shape=jax.ShapeDtypeStruct((rows, kr), bf16),
        in_specs=[hbm] * 7,
        out_specs=hbm,
        scratch_shapes=[
            pltpu.VMEM((2 * ring, kr, sc), bf16),
            pltpu.VMEM((n_t, pieces, rows, kr // pieces), bf16),
            pltpu.VMEM((1, width), f32),
            pltpu.VMEM((2, rows), i32),
            pltpu.VMEM((2, rows), f32),
            pltpu.VMEM((slots, rows), bf16),
            pltpu.VMEM((rows, slots), bf16),
            pltpu.VMEM((slots, LANES), f32),
            pltpu.VMEM((slots, LANES), f32),
            pltpu.VMEM((n_t, pieces, slots, kr // pieces), bf16),
            pltpu.VMEM((n_t, pieces, slots, kr // pieces), bf16),
            pltpu.VMEM((pieces, slots, kr // pieces), bf16),
            pltpu.VMEM((slots, LANES), f32),
            pltpu.VMEM((slots, LANES), f32),
            pltpu.VMEM((slots, hid), f32),
            pltpu.VMEM((slots, hid), f32),
            pltpu.VMEM((slots, hid), bf16),
            pltpu.VMEM((down_chunks, slots, dc), bf16),
            pltpu.VMEM((down_chunks, slots, dc), bf16),
            pltpu.VMEM((down_chunks, rows, dc), bf16),
            pltpu.VMEM((2, n_t // 2, per_slice, rows, dc), bf16),
            pltpu.VMEM((rows, kr), bf16),
            dma((2 * ring, sc // dc)),
            dma((3 + pieces + per_slice,)),
            dma((n_t, pieces)),
            dma((n_t, pieces)),
            dma((n_e, n_t, pieces)),
            dma((n_t, pieces, n_e)),
            dma((n_e,)),
            dma((n_e,)),
            dma((n_e, down_chunks)),
            dma((down_chunks, n_e)),
            dma((down_chunks,)),
            dma((2, n_t // 2, per_slice)),
        ],
        compiler_params=pltpu.CompilerParams(
            collective_id=0, has_side_effects=True, vmem_limit_bytes=67043328
        ),
    )(tokens, norm_gain.reshape(1, width), expert_ids.T, gate_weights.T, w_gate, w_up, w_down)


def solution(mesh):
    in_specs = (
        P(("groups", "expert"), "tensor"),
        P(),
        P(None, ("expert", "tensor")),
        P(None, ("expert", "tensor")),
        P(("expert", "tensor"), None),
        P(("groups", "expert"), None),
        P(("groups", "expert"), None),
    )
    out_specs = P(("groups", "expert"), "tensor")
    body = functools.partial(per_device, mesh.shape["expert"], mesh.shape["tensor"])
    return jax.shard_map(body, mesh=mesh, in_specs=in_specs, out_specs=out_specs, check_vma=False)
```

time: 60.5 us -> 48.6 us (0.80); the launches traced: 59.6 us -> 48.5 us
  Pallas kernels: 54.7 us -> 46.9 us
  other arithmetic: 1.95 us -> 0 us
  local copies, waits for them, and re-layouts: 2.95 us -> 1.57 us
    pallas_call x1, Pallas kernels: 54.7 us -> 46.9 us  [per_device(): pl.pallas_call(functools.partial(kernel, n_e, n_t, cap, ring, 3, pieces,...]
    unnamed x2 -> x1, local copies, waits for them, and re-layouts: 2.95 us -> 1.57 us
    concatenate x1 -> x0, other arithmetic: 1.27 us -> none  [per_device(): jnp.concatenate([jnp.pad(expert_ids.T.astype(jnp.float32), ((0, 0), (0, p...]
    convert_element_type x1 -> x0, other arithmetic: 0.68 us -> none  [per_device(): expert_ids.T.astype(jnp.float32)]
where the time goes in v1:
time: 48.6 us; the launch traced here: 48.5 us
  Pallas kernels  46.9 us (97%)
  local copies, waits for them, and re-layouts  1.57 us (3%)
    pallas_call x1, Pallas kernels, per_device(): pl.pallas_call(functools.partial(kernel, n_e, n_t, cap, ring, 3, pieces,...  46.9 us
    unnamed x1, local copies, waits for them, and re-layouts  1.57 us

profile of v1, /device:TPU:0, one launch (start us, length us, event | category | flops | bytes accessed | tf_op | source)
XLA Modules:
  0.0 48.5 jit_solution(14552478193944243053)
XLA Ops:
  0.0 46.9 %shard_map.73 = bf16[64,1024]{1,0:T(8,128)(2,1)} custom-call(bf16[64,1024]{1,0:T(8,128)(2,1)} %tokens.1, f32[1,4096]{1,0:T(1,128)} %bitcast.3, s32[2,64]{1,0:T(2,128)} %bitcast.4, f32[2,64]{1,0:T(2,128)} %bitcast.5, bf16[4096,4096]{1,0:T(8,128)(2,1)} %w_gate.1, bf16[4096,4096]{1,0:T(8,128)(2,1)} %w_up.1, bf16[4096,4096]{1,0:T(8,128)(2,1)} %w_down.1), custom_call_target="tpu_custom_call" | custom-call | tf_op jit(solution)/shard_map/pallas_call | solution.py:410
  46.9 1.6 %copy.9 = bf16[64,1024]{1,0:T(8,128)(2,1)} copy(bf16[64,1024]{1,0:T(8,128)(2,1)} %shard_map.73) | data formatting | bytes 262144

commit v2 on v1

--- a/solution.py
+++ b/solution.py
@@ -19,7 +19,7 @@
     out,
     wbuf, blocks, gain, ids, weights, spread, place, wsend, wslot, sendpk, recvpk, packed, ssq, scale,
     acc_gate, acc_up, hidden,
-    sendbuf, recvbuf, zsend, zrecv, outbuf,
+    sendbuf, recvbuf, zsend, zrecv,
     wsem, lsem, rsem, zsem, psend, precv, msend, mrecv, osend, orecv, ysend, yrecv,
 ):
     g, e, t = lax.axis_index("groups"), lax.axis_index("expert"), lax.axis_index("tensor")
@@ -116,12 +116,12 @@
     own_rows = columns(e * cap, cap)
 
     local = [
+        pltpu.make_async_copy(tokens.at[:, p * kp:(p + 1) * kp], blocks.at[t, p], lsem.at[3 + p])
+        for p in range(pieces)
+    ] + [
         pltpu.make_async_copy(ids_in, ids, lsem.at[0]),
         pltpu.make_async_copy(weights_in, weights, lsem.at[1]),
         pltpu.make_async_copy(gain_in, gain, lsem.at[2]),
-    ] + [
-        pltpu.make_async_copy(tokens.at[:, p * kp:(p + 1) * kp], blocks.at[t, p], lsem.at[3 + p])
-        for p in range(pieces)
     ]
     for copy in local:
         copy.start()
@@ -135,14 +135,24 @@
         start_unit(u)
         return 0
 
-    lax.fori_loop(0, min(ring, units), prefetch, 0)
-    for copy in local:
+    early = min(ring, units, 4)
+    lax.fori_loop(0, early, prefetch, 0)
+    for p in range(pieces):
+        local[p].wait()
+    pl.semaphore_wait(barrier, n_e - 1 + n_t - 1)
+    for p in range(pieces):
+        z_copy(1, p).start()
+    for j in range(2, n_t, 2):
+        for p in range(pieces):
+            z_copy(j, p).start()
+    for copy in local[pieces:]:
         copy.wait()
 
     upper = (
         lax.broadcasted_iota(jnp.int32, (rows, rows), 0) < lax.broadcasted_iota(jnp.int32, (rows, rows), 1)
     ).astype(jnp.float32).astype(jnp.bfloat16)
 
+    hits = []
     for ej in range(n_e):
         expert = (ej * n_t + t) // per_expert
         named = jnp.where(ids[0:1, :] == expert, 1.0, 0.0) + jnp.where(ids[1:2, :] == expert, 1.0, 0.0)
@@ -150,17 +160,8 @@
             jnp.broadcast_to(named, (8, rows)).astype(jnp.bfloat16), upper, preferred_element_type=jnp.float32
         )[0:1, :]
         slot = lax.broadcasted_iota(jnp.int32, (cap, rows), 0).astype(jnp.float32)
-        hit = jnp.where(slot == rank, 1.0, 0.0) * named
-        weight = jnp.where(ids[0:1, :] == expert, weights[0:1, :], weights[1:2, :])
-        at = slice(ej * cap, (ej + 1) * cap)
-        spread[at, :] = hit.astype(jnp.bfloat16)
-        wsend[at, :] = jnp.broadcast_to(jnp.sum(hit * weight, axis=1, keepdims=True), (cap, LANES))
-        filled = jnp.concatenate([hit, jnp.zeros((cap, LANES - rows), jnp.float32)], axis=1)
-        place[:, at] = jnp.transpose(filled)[0:rows, :].astype(jnp.bfloat16)
-    wslot[own_rows, :] = wsend[own_rows, :]
-    ssq[...] = jnp.zeros_like(ssq)
-
-    pl.semaphore_wait(barrier, n_e - 1 + n_t - 1)
+        hits.append(jnp.where(slot == rank, 1.0, 0.0) * named)
+        spread[ej * cap:(ej + 1) * cap, :] = hits[ej].astype(jnp.bfloat16)
 
     def dispatch(q, p):
         picked = jnp.dot(spread[...], blocks[q, p], preferred_element_type=jnp.float32)
@@ -245,12 +246,17 @@
         lax.fori_loop(0, nj, one, 0)
 
     for p in range(pieces):
-        z_copy(1, p).start()
-    for j in range(2, n_t, 2):
-        for p in range(pieces):
-            z_copy(j, p).start()
-    for p in range(pieces):
         dispatch(t, p)
+    lax.fori_loop(early, min(ring, units), prefetch, 0)
+    for ej in range(n_e):
+        expert = (ej * n_t + t) // per_expert
+        weight = jnp.where(ids[0:1, :] == expert, weights[0:1, :], weights[1:2, :])
+        at = slice(ej * cap, (ej + 1) * cap)
+        wsend[at, :] = jnp.broadcast_to(jnp.sum(hits[ej] * weight, axis=1, keepdims=True), (cap, LANES))
+        filled = jnp.concatenate([hits[ej], jnp.zeros((cap, LANES - rows), jnp.float32)], axis=1)
+        place[:, at] = jnp.transpose(filled)[0:rows, :].astype(jnp.bfloat16)
+    wslot[own_rows, :] = wsend[own_rows, :]
+    ssq[...] = jnp.zeros_like(ssq)
     take(jnp.int32(1))
     expert_in(jnp.int32(0), True, False)
 
@@ -343,18 +349,12 @@
         return 0
 
     lax.fori_loop(max(0, down_chunks - lag), down_chunks - per_slice, late, 0)
-    results = []
     for c in range(per_slice):
         total = combined(down_chunks - per_slice + c)
         total += y_arrived(0, 0, c)
         for m in range(1, n_t // 2):
             total += y_arrived(1, m, c)
-        outbuf[:, c * dc:(c + 1) * dc] = total.astype(jnp.bfloat16)
-        done = pltpu.make_async_copy(
-            outbuf.at[:, c * dc:(c + 1) * dc], out.at[:, c * dc:(c + 1) * dc], lsem.at[3 + pieces + c]
-        )
-        done.start()
-        results.append(done)
+        out[:, c * dc:(c + 1) * dc] = total.astype(jnp.bfloat16)
 
     for o in range(1, n_e):
         m_copy(o).wait_send()
@@ -383,8 +383,6 @@
         return 0
 
     lax.fori_loop(0, down_chunks - per_slice, drain_sums, 0)
-    for done in results:
-        done.wait()
 
 
 def per_device(n_e, n_t, tokens, norm_gain, w_gate, w_up, w_down, expert_ids, gate_weights):
@@ -400,6 +398,7 @@
     per_slice = kr // dc
     down_chunks = n_t * per_slice
     units = n_t * (hid // sc) + down_chunks
+    out_bytes = max(2 * rows * kr, MIB // 4)
     spent = (
         6 * rows * width + 8 * slots * width + 2 * slots * kr + 10 * slots * hid
         + 18 * slots * LANES + 2 * rows * kr + MIB
@@ -408,10 +407,10 @@
     hbm = pl.BlockSpec(memory_space=pl.ANY)
     bf16, f32, i32, dma = jnp.bfloat16, jnp.float32, jnp.int32, pltpu.SemaphoreType.DMA
     return pl.pallas_call(
-        functools.partial(kernel, n_e, n_t, cap, ring, 3, pieces, dc),
-        out_shape=jax.ShapeDtypeStruct((rows, kr), bf16),
+        functools.partial(kernel, n_e, n_t, cap, ring, 2, pieces, dc),
+        out_shape=pltpu.VMEM((rows, kr), bf16),
         in_specs=[hbm] * 7,
-        out_specs=hbm,
+        out_specs=pl.BlockSpec(memory_space=pltpu.VMEM),
         scratch_shapes=[
             pltpu.VMEM((2 * ring, kr, sc), bf16),
             pltpu.VMEM((n_t, pieces, rows, kr // pieces), bf16),
@@ -434,9 +433,8 @@
             pltpu.VMEM((down_chunks, slots, dc), bf16),
             pltpu.VMEM((down_chunks, rows, dc), bf16),
             pltpu.VMEM((2, n_t // 2, per_slice, rows, dc), bf16),
-            pltpu.VMEM((rows, kr), bf16),
             dma((2 * ring, sc // dc)),
-            dma((3 + pieces + per_slice,)),
+            dma((3 + pieces,)),
             dma((n_t, pieces)),
             dma((n_t, pieces)),
             dma((n_e, n_t, pieces)),
@@ -449,7 +447,7 @@
             dma((2, n_t // 2, per_slice)),
         ],
         compiler_params=pltpu.CompilerParams(
-            collective_id=0, has_side_effects=True, vmem_limit_bytes=67043328
+            collective_id=0, has_side_effects=True, vmem_limit_bytes=67043328 - 2 * out_bytes
         ),
     )(tokens, norm_gain.reshape(1, width), expert_ids.T, gate_weights.T, w_gate, w_up, w_down)
 

time: 48.6 us -> 46.1 us (0.949)
  Pallas kernels: 46.9 us -> 45.3 us
  local copies, waits for them, and re-layouts: 1.57 us -> 0.66 us
    pallas_call x1, Pallas kernels: 46.9 us -> 45.3 us  [per_device(): pl.pallas_call(functools.partial(kernel, n_e, n_t, cap, ring, 2, pieces,...]
    unnamed x1, local copies, waits for them, and re-layouts: 1.57 us -> 0.66 us
where the time goes in v2:
time: 46.1 us; the launch traced here: 45.9 us
  Pallas kernels  45.3 us (98%)
  local copies, waits for them, and re-layouts  0.66 us (1%)
    pallas_call x1, Pallas kernels, per_device(): pl.pallas_call(functools.partial(kernel, n_e, n_t, cap, ring, 2, pieces,...  45.3 us

profile of v2, /device:TPU:0, one launch (start us, length us, event | category | flops | bytes accessed | tf_op | source)
XLA Modules:
  0.0 45.9 jit_solution(6112863493277824996)
XLA Ops:
  0.0 45.3 %shard_map.73 = bf16[64,1024]{1,0:T(8,128)(2,1)S(1)} custom-call(bf16[64,1024]{1,0:T(8,128)(2,1)} %tokens.1, f32[1,4096]{1,0:T(1,128)} %bitcast.3, s32[2,64]{1,0:T(2,128)} %bitcast.4, f32[2,64]{1,0:T(2,128)} %bitcast.5, bf16[4096,4096]{1,0:T(8,128)(2,1)} %w_gate.1, bf16[4096,4096]{1,0:T(8,128)(2,1)} %w_up.1, bf16[4096,4096]{1,0:T(8,128)(2,1)} %w_down.1), custom_call_target="tpu_custom_call" | custom-call | tf_op jit(solution)/shard_map/pallas_call | solution.py:409
  45.3 0.7 %copy.9 = bf16[64,1024]{1,0:T(8,128)(2,1)} copy(bf16[64,1024]{1,0:T(8,128)(2,1)S(1)} %shard_map.73) | data formatting | bytes 262144

commit v3 on v2

--- a/solution.py
+++ b/solution.py
@@ -349,40 +349,41 @@
         return 0
 
     lax.fori_loop(max(0, down_chunks - lag), down_chunks - per_slice, late, 0)
+    for o in range(1, n_e):
+        m_copy(o).wait_send()
+
+    for j in range(1, n_t):
+        for p in range(pieces):
+            z_copy(j, p).wait_send()
+
+    def drain_blocks(s, _):
+        for p in range(pieces):
+            for o in range(1, n_e):
+                p_copy(o, s, p).wait_send()
+        return 0
+
+    lax.fori_loop(0, n_t, drain_blocks, 0)
+
     for c in range(per_slice):
+        if c == per_slice - 1:
+            def drain_rows(d, _):
+                for o in range(1, n_e):
+                    o_copy(o, d).wait_send()
+                return 0
+
+            lax.fori_loop(0, down_chunks, drain_rows, 0)
+
+            def drain_sums(d, _):
+                y_copy(d, 0).wait_send()
+                return 0
+
+            lax.fori_loop(0, down_chunks - per_slice, drain_sums, 0)
+
         total = combined(down_chunks - per_slice + c)
         total += y_arrived(0, 0, c)
         for m in range(1, n_t // 2):
             total += y_arrived(1, m, c)
         out[:, c * dc:(c + 1) * dc] = total.astype(jnp.bfloat16)
-
-    for o in range(1, n_e):
-        m_copy(o).wait_send()
-
-    for j in range(1, n_t):
-        for p in range(pieces):
-            z_copy(j, p).wait_send()
-
-    def drain_blocks(s, _):
-        for p in range(pieces):
-            for o in range(1, n_e):
-                p_copy(o, s, p).wait_send()
-        return 0
-
-    lax.fori_loop(0, n_t, drain_blocks, 0)
-
-    def drain_rows(d, _):
-        for o in range(1, n_e):
-            o_copy(o, d).wait_send()
-        return 0
-
-    lax.fori_loop(0, down_chunks, drain_rows, 0)
-
-    def drain_sums(d, _):
-        y_copy(d, 0).wait_send()
-        return 0
-
-    lax.fori_loop(0, down_chunks - per_slice, drain_sums, 0)
 
 
 def per_device(n_e, n_t, tokens, norm_gain, w_gate, w_up, w_down, expert_ids, gate_weights):

time: 46.1 us -> 45.9 us (level)
  no operation moved by 1% of the time
where the time goes in v3:
time: 45.9 us; the launch traced here: 45.8 us
  Pallas kernels  45.1 us (98%)
  local copies, waits for them, and re-layouts  0.66 us (1%)
    pallas_call x1, Pallas kernels, per_device(): pl.pallas_call(functools.partial(kernel, n_e, n_t, cap, ring, 2, pieces,...  45.1 us

profile of v3, /device:TPU:0, one launch (start us, length us, event | category | flops | bytes accessed | tf_op | source)
XLA Modules:
  0.0 45.8 jit_solution(16931932797763053306)
XLA Ops:
  0.0 45.1 %shard_map.73 = bf16[64,1024]{1,0:T(8,128)(2,1)S(1)} custom-call(bf16[64,1024]{1,0:T(8,128)(2,1)} %tokens.1, f32[1,4096]{1,0:T(1,128)} %bitcast.3, s32[2,64]{1,0:T(2,128)} %bitcast.4, f32[2,64]{1,0:T(2,128)} %bitcast.5, bf16[4096,4096]{1,0:T(8,128)(2,1)} %w_gate.1, bf16[4096,4096]{1,0:T(8,128)(2,1)} %w_up.1, bf16[4096,4096]{1,0:T(8,128)(2,1)} %w_down.1), custom_call_target="tpu_custom_call" | custom-call | tf_op jit(solution)/shard_map/pallas_call | solution.py:410
  45.1 0.7 %copy.9 = bf16[64,1024]{1,0:T(8,128)(2,1)} copy(bf16[64,1024]{1,0:T(8,128)(2,1)S(1)} %shard_map.73) | data formatting | bytes 262144
